TPU v7x, 32 devices: a whole 2x2x4 slice. The times are simulated.
32 devices in a mesh: grid: 2 (over x), prow: 4 (over y, core), pcol: 4 (over z).
Axes of the slice: x: 2, y: 2, z: 4, core: 2. Of those that a mesh axis runs over, the one named last changes fastest.
Arguments:
- sub_rhs: float32 [2, 3, 64, 3072], P('grid', None, None, 'prow'), may hold values from -6 to 6
- root_rhs: float32 [64, 3072], P(None, 'prow'), may hold values from -6 to 6
- diag_inverse: bfloat16 [3, 3072, 6144], P(None, 'prow', ('grid', 'pcol'))
- root_inverse: bfloat16 [3072, 3072], P('prow', 'grid')
- inner_factor: bfloat16 [3, 6144, 3072], P(None, ('grid', 'pcol'), 'prow'), may hold values from -0.078125 to 0.078125
- inner_mask: int32 [3, 48, 24], P(None, ('grid', 'pcol')), may hold values 0 or 1
- root_factor: bfloat16 [3, 6144, 3072], P(None, ('grid', 'pcol'), 'prow'), may hold values from -0.078125 to 0.078125
- root_mask: int32 [3, 48, 24], P(None, ('grid', 'pcol')), may hold values 0 or 1
Outputs:
- sub_solution: float32 [3, 64, 6144], P(None, None, ('grid', 'pcol'))
- root_solution: float32 [64, 3072], P(None, 'grid')
Inputs may be any that keep to these rules, and one draw needn't show every extreme that they name: `inner_mask`: 1 keeps a tile of 128 x 128 entries, 0 makes it zero. `root_mask`: 1 keeps a tile of 128 x 128 entries, 0 makes it zero.
All inputs are finite; a program needn't handle non-finite values. No bound on the sum of `inner_mask` or of `root_mask` on one device may be relied on, other than what follows from the above.
Results may differ from a plain program's by a relative error of at most 0.0065.
Values sent between devices are 32-bit elements; how exact they have to be, the bound alone decides.
A program may use at most 64 MiB of HBM per device.

v0:
```python
import jax
import jax.numpy as jnp
from jax import lax
from jax.sharding import PartitionSpec as P

NS = 3072
LEVELS = 3
TILE = 128


def from_partner(shard, axis, bit):
    return lax.ppermute(shard, axis, [(i, i ^ 1 << bit) for i in range(lax.axis_size(axis))])


def selector(positions, count):
    return (positions[:, None] // TILE == jnp.arange(count)[None, :]).astype(jnp.float32)


def masked(factor, mask, row_select, col_select):
    expanded = jnp.dot(jnp.dot(row_select, mask.astype(jnp.float32)), col_select.T)
    return factor * expanded.astype(jnp.bfloat16)


def solve_block(residual, inverse):
    partial_sum = jnp.dot(
        residual.astype(jnp.bfloat16), inverse, preferred_element_type=jnp.float32
    )
    return lax.psum(partial_sum, "prow")


def group_sum(partial_sum, owners):
    summed = partial_sum
    for bit_number in range(owners.bit_length() - 1):
        summed = summed + from_partner(summed, "pcol", bit_number)
    return summed


def shards(
    sub_rhs, root_rhs, diag_inverse, root_inverse, inner_factor, inner_mask, root_factor, root_mask
):
    rows_here = inner_factor.shape[1]
    out_cols = inner_factor.shape[2]
    owners = NS // rows_here
    own_tree = lax.axis_index("pcol") // owners
    col_positions = lax.axis_index("prow") * out_cols + jnp.arange(out_cols)
    row_select = selector(jnp.arange(rows_here), inner_mask.shape[1])
    col_select = selector(col_positions, inner_mask.shape[2])
    own_rhs = lax.dynamic_index_in_dim(sub_rhs, own_tree, 0, keepdims=False)
    kept = []
    solved_all = []
    pair = 0
    for level in range(LEVELS):
        residual = own_rhs[level]
        if level > 0:
            local_update = jnp.zeros(residual.shape, jnp.float32)
            for source in range(level):
                factor_tile = masked(inner_factor[pair], inner_mask[pair], row_select, col_select)
                local_update = local_update + jnp.dot(
                    kept[source], factor_tile, preferred_element_type=jnp.float32
                )
                pair += 1
            residual = residual - group_sum(local_update, owners)
        solved = solve_block(residual, diag_inverse[level])
        solved_all.append(solved)
        kept.append(solved.astype(jnp.bfloat16))
    root_local = jnp.zeros(root_rhs.shape, jnp.float32)
    for source in range(LEVELS):
        factor_tile = masked(root_factor[source], root_mask[source], row_select, col_select)
        root_local = root_local + jnp.dot(
            kept[source], factor_tile, preferred_element_type=jnp.float32
        )
    across = lax.psum(root_local, "pcol")
    root_update = lax.psum(across, "grid")
    root_solution = solve_block(root_rhs - root_update, root_inverse)
    return (jnp.stack(solved_all), root_solution)


def solution(mesh):
    return jax.shard_map(
        shards,
        mesh=mesh,
        in_specs=(
            P("grid", None, None, "prow"),
            P(None, "prow"),
            P(None, "prow", ("grid", "pcol")),
            P("prow", "grid"),
            P(None, ("grid", "pcol"), "prow"),
            P(None, ("grid", "pcol"), None),
            P(None, ("grid", "pcol"), "prow"),
            P(None, ("grid", "pcol"), None),
        ),
        out_specs=(P(None, None, ("grid", "pcol")), P(None, "grid")),
        check_vma=False,
    )
```

profile of v0, /device:TPU:0, one launch (start us, length us, event | category | flops | bytes accessed | tf_op | source)
XLA Modules:
  0.0 262.5 jit_solution(7148002226130458398)
XLA Ops:
  7.2 2.5 fusion.22
  11.0 34.6 %all-reduce.7.cloned.1.call-done = f32[64,768]{1,0:T(8,128)} async-done(((f32[64,768]{1,0:T(8,128)}), f32[64,768]{1,0:T(8,128)}) %all-reduce.7.cloned.1.call-update) | async-done | bytes 196624 | tf_op jit(solution)/shard_map/psum | solution.py:28
  45.7 2.1 fusion.11
  50.3 3.2 %collective-permute-done = f32[64,768]{1,0:T(8,128)S(1)} collective-permute-done((f32[64,768]{1,0:T(8,128)S(1)}, f32[64,768]{1,0:T(8,128)S(1)}, u32[]{:S(2)}, u32[]{:S(2)}) %collective-permute-start) | collective-permute-done | bytes 196640 | tf_op jit(solution)/shard_map/ppermute | solution.py:12
  53.6 2.5 collective-permute-start.1
  56.0 1.7 fusion.37
  57.7 5.2 %collective-permute-done.1 = f32[64,768]{1,0:T(8,128)S(1)} collective-permute-done((f32[64,768]{1,0:T(8,128)S(1)}, f32[64,768]{1,0:T(8,128)S(1)}, u32[]{:S(2)}, u32[]{:S(2)}) %collective-permute-start.1) | collective-permute-done | bytes 196640 | tf_op jit(solution)/shard_map/ppermute | solution.py:12
  62.9 2.3 fusion.19
  66.3 32.6 %all-reduce.9.cloned.1.call-done = f32[64,768]{1,0:T(8,128)} async-done(((f32[64,768]{1,0:T(8,128)}), f32[64,768]{1,0:T(8,128)}) %all-reduce.9.cloned.1.call-update) | async-done | bytes 196624 | tf_op jit(solution)/shard_map/psum | solution.py:28
  98.8 2.8 %fusion.9 = f32[64,768]{1,0:T(8,128)} fusion(bf16[768,24]{1,0:T(8,128)(2,1)S(1)} %fusion.39, bf16[3,768,768]{2,1,0:T(8,128)(2,1)} %param.12, s32[768]{0:T(1024)S(1)} %copy-done.10, f32[64,768]{1,0:T(8,128)} %all-reduce.9.cloned.1.call-done), kind=kOutput, calls=%fused_computation.15 | convolution fusion | flops 104466432 | bytes 1612800 | tf_op jit(solution)/shard_map/dot_general | solution.py:58
  101.7 2.2 fusion.33
  106.4 3.2 %collective-permute-done.2 = f32[64,768]{1,0:T(8,128)S(1)} collective-permute-done((f32[64,768]{1,0:T(8,128)S(1)}, f32[64,768]{1,0:T(8,128)S(1)}, u32[]{:S(2)}, u32[]{:S(2)}) %collective-permute-start.2) | collective-permute-done | bytes 196640 | tf_op jit(solution)/shard_map/ppermute | solution.py:12
  110.6 2.5 collective-permute-start.3
  113.0 2.8 %fusion.7 = f32[64,768]{1,0:T(8,128)} fusion(bf16[768,24]{1,0:T(8,128)(2,1)} %fusion.37, bf16[3,768,768]{2,1,0:T(8,128)(2,1)} %param.14, s32[768]{0:T(1024)} %add_select_fusion, f32[64,768]{1,0:T(8,128)S(1)} %copy-done.4), kind=kOutput, calls=%fused_computation.13 | convolution fusion | flops 104466432 | bytes 1773568 | tf_op jit(solution)/shard_map/dot_general | solution.py:69
  115.9 4.1 %collective-permute-done.3 = f32[64,768]{1,0:T(8,128)} collective-permute-done((f32[64,768]{1,0:T(8,128)S(1)}, f32[64,768]{1,0:T(8,128)}, u32[]{:S(2)}, u32[]{:S(2)}) %collective-permute-start.3) | collective-permute-done | bytes 196640 | tf_op jit(solution)/shard_map/ppermute | solution.py:12
  120.0 2.4 fusion.15
  122.5 2.1 fusion.34
  124.6 31.4 %all-reduce.11.cloned.1.call-done = f32[64,768]{1,0:T(8,128)} async-done(((f32[64,768]{1,0:T(8,128)}), f32[64,768]{1,0:T(8,128)}) %all-reduce.11.cloned.1.call-update) | async-done | bytes 196624 | tf_op jit(solution)/shard_map/psum | solution.py:28
  156.0 2.8 %fusion.35 = f32[64,768]{1,0:T(8,128)} fusion(f32[64,768]{1,0:T(8,128)S(1)} %fusion.34, bf16[768,24]{1,0:T(8,128)(2,1)S(1)} %copy-done.6, bf16[3,768,768]{2,1,0:T(8,128)(2,1)} %param.14, s32[768]{0:T(1024)S(1)} %copy-done.11, f32[64,768]{1,0:T(8,128)} %all-reduce.11.cloned.1.call-done), kind=kOutput, calls=%fused_computation.41 | convolution fusion | flops 104515584 | bytes 1809408 | tf_op jit(solution)/shard_map/dot_general | solution.py:69
  158.9 35.1 %all-reduce.13.cloned.1.call-done = f32[64,768]{1,0:T(8,128)} async-done(((f32[64,768]{1,0:T(8,128)}), f32[64,768]{1,0:T(8,128)}) %all-reduce.13.cloned.1.call-update) | async-done | bytes 196624 | tf_op jit(solution)/shard_map/psum | solution.py:72
  194.1 24.1 %all-reduce.15.cloned.1.call-done = f32[64,768]{1,0:T(8,128)} async-done(((f32[64,768]{1,0:T(8,128)}), f32[64,768]{1,0:T(8,128)}) %all-reduce.15.cloned.1.call-update) | async-done | bytes 196624 | tf_op jit(solution)/shard_map/psum | solution.py:73
  218.3 2.2 fusion.62
  221.4 32.5 %all-reduce.17.cloned.1.call-done = f32[64,1536]{1,0:T(8,128)} async-done(((f32[64,1536]{1,0:T(8,128)}), f32[64,1536]{1,0:T(8,128)}) %all-reduce.17.cloned.1.call-update) | async-done | bytes 393232 | tf_op jit(solution)/shard_map/psum | solution.py:28
  253.9 1.8 copy.16
  (48 shorter events, 9.4 us)
Async XLA Ops:
  7.2 211.1 %copy-start = (bf16[768,1536]{1,0:T(8,128)(2,1)S(1)}, bf16[768,1536]{1,0:T(8,128)(2,1)}, u32[]{:S(2)}) copy-start(bf16[768,1536]{1,0:T(8,128)(2,1)} %param.11) | copy-start | bytes 7077892
  7.2 2.7 %copy-start.8 = (s32[3,6,24]{2,1,0:T(8,128)S(1)}, s32[3,6,24]{2,1,0:T(8,128)}, u32[]{:S(2)}) copy-start(s32[3,6,24]{2,1,0:T(8,128)} %param.13) | copy-start | bytes 5188
  7.2 38.5 %all-reduce.7.cloned.1.call-start = ((), (), s32[]{:S(2)}) async-start(), calls=%async_computation | async-start | bytes 393216 | tf_op jit(solution)/shard_map/psum | solution.py:28
  9.8 89.0 %all-reduce.9.cloned.1.call-start = ((), (), s32[]{:S(2)}) async-start(), calls=%async_computation.1 | async-start | bytes 393216 | tf_op jit(solution)/shard_map/psum | solution.py:28
  11.0 51.9 %copy-start.1 = (f32[1,3,64,768]{3,2,1,0:T(8,128)S(1)}, f32[1,3,64,768]{3,2,1,0:T(8,128)}, u32[]{:S(2)}) copy-start(f32[1,3,64,768]{3,2,1,0:T(8,128)} %param.8) | copy-start | bytes 1769476
  47.8 5.7 %collective-permute-start = (f32[64,768]{1,0:T(8,128)S(1)}, f32[64,768]{1,0:T(8,128)S(1)}, u32[]{:S(2)}, u32[]{:S(2)}) collective-permute-start(f32[64,768]{1,0:T(8,128)S(1)} %fusion.11), channel_id=1, source_target_pairs={{0,1},{1,0},{2,3},{3,2},{4,5},{5,4},{6,7},{7,6},{8,9},{9,8},{10,11... | collective-permute-start | bytes 589832 | tf_op jit(solution)/shard_map/ppermute | solution.py:12
  53.6 11.7 %copy-start.9 = (s32[3,6,24]{2,1,0:T(8,128)S(1)}, s32[3,6,24]{2,1,0:T(8,128)}, u32[]{:S(2)}) copy-start(s32[3,6,24]{2,1,0:T(8,128)} %param.15) | copy-start | bytes 5188
  53.6 9.4 %collective-permute-start.1 = (f32[64,768]{1,0:T(8,128)S(1)}, f32[64,768]{1,0:T(8,128)S(1)}, u32[]{:S(2)}, u32[]{:S(2)}) collective-permute-start(f32[64,768]{1,0:T(8,128)S(1)} %add.60), channel_id=1, source_target_pairs={{0,2},{1,3},{2,0},{3,1},{4,6},{5,7},{6,4},{7,5},{8,10},{9,11},{10,... | collective-permute-start | bytes 589832 | tf_op jit(solution)/shard_map/ppermute | solution.py:12
  57.7 41.1 %copy-start.10 = (s32[768]{0:T(1024)S(1)}, s32[768]{0:T(1024)}, u32[]{:S(2)}) copy-start(s32[768]{0:T(1024)} %add_select_fusion) | copy-start | bytes 9220
  65.2 36.4 %copy-start.3 = (f32[64,768]{1,0:T(8,128)S(1)}, f32[64,768]{1,0:T(8,128)}, u32[]{:S(2)}) copy-start(f32[64,768]{1,0:T(8,128)} %all-reduce.7.cloned.1.call-done) | copy-start | bytes 589828
  65.2 90.8 %all-reduce.11.cloned.1.call-start = ((), (), s32[]{:S(2)}) async-start(), calls=%async_computation.2 | async-start | bytes 393216 | tf_op jit(solution)/shard_map/psum | solution.py:28
  101.7 11.4 %copy-start.4 = (f32[64,768]{1,0:T(8,128)S(1)}, f32[64,768]{1,0:T(8,128)}, u32[]{:S(2)}) copy-start(f32[64,768]{1,0:T(8,128)} %all-reduce.9.cloned.1.call-done) | copy-start | bytes 589828
  103.9 2.5 copy-start.7
  103.9 5.7 %collective-permute-start.2 = (f32[64,768]{1,0:T(8,128)S(1)}, f32[64,768]{1,0:T(8,128)S(1)}, u32[]{:S(2)}, u32[]{:S(2)}) collective-permute-start(f32[64,768]{1,0:T(8,128)S(1)} %fusion.33), channel_id=1, source_target_pairs={{0,1},{1,0},{2,3},{3,2},{4,5},{5,4},{6,7},{7,6},{8,9},{9,8},{10,11... | collective-permute-start | bytes 589832 | tf_op jit(solution)/shard_map/ppermute | solution.py:12
  110.6 9.5 %collective-permute-start.3 = (f32[64,768]{1,0:T(8,128)S(1)}, f32[64,768]{1,0:T(8,128)}, u32[]{:S(2)}, u32[]{:S(2)}) collective-permute-start(f32[64,768]{1,0:T(8,128)S(1)} %add.63), channel_id=1, source_target_pairs={{0,2},{1,3},{2,0},{3,1},{4,6},{5,7},{6,4},{7,5},{8,10},{9,11},{10,... | collective-permute-start | bytes 589832 | tf_op jit(solution)/shard_map/ppermute | solution.py:12
  115.9 6.6 %copy-start.11 = (s32[768]{0:T(1024)S(1)}, s32[768]{0:T(1024)}, u32[]{:S(2)}) copy-start(s32[768]{0:T(1024)} %add_select_fusion) | copy-start | bytes 9220
  122.4 33.6 %copy-start.6 = (bf16[768,24]{1,0:T(8,128)(2,1)S(1)}, bf16[768,24]{1,0:T(8,128)(2,1)}, u32[]{:S(2)}) copy-start(bf16[768,24]{1,0:T(8,128)(2,1)} %fusion.36) | copy-start | bytes 110596
  122.4 71.6 %all-reduce.13.cloned.1.call-start = ((), (), s32[]{:S(2)}) async-start(), calls=%async_computation.3 | async-start | bytes 393216 | tf_op jit(solution)/shard_map/psum | solution.py:72
  124.6 93.6 %copy-start.2 = (f32[64,768]{1,0:T(8,128)S(1)}, f32[64,768]{1,0:T(8,128)}, u32[]{:S(2)}) copy-start(f32[64,768]{1,0:T(8,128)} %param.9) | copy-start | bytes 589828
  158.9 59.4 %all-reduce.15.cloned.1.call-start = ((), (), s32[]{:S(2)}) async-start(), calls=%async_computation.4 | async-start | bytes 393216 | tf_op jit(solution)/shard_map/psum | solution.py:73
  194.1 26.4 %copy-start.5 = (f32[64,768]{1,0:T(8,128)S(1)}, f32[64,768]{1,0:T(8,128)}, u32[]{:S(2)}) copy-start(f32[64,768]{1,0:T(8,128)} %all-reduce.11.cloned.1.call-done) | copy-start | bytes 589828
  194.1 59.8 %all-reduce.17.cloned.1.call-start = ((), (), s32[]{:S(2)}) async-start(), calls=%async_computation.5 | async-start | bytes 786432 | tf_op jit(solution)/shard_map/psum | solution.py:28
Sparse Core Ops, SparseCore 0:
  10.9 34.7 all-reduce.6
  65.3 33.4 all-reduce.8
  122.6 33.4 all-reduce.10
  159.0 34.9 all-reduce.12
  196.2 22.0 all-reduce.14
  221.1 32.7 all-reduce.16
where the time goes:
time: 263 us
  waiting for transfers between devices  206 us (78%)
  matrix products  29.5 us (11%)
  between operations  14.3 us (5%)
  starting transfers between devices  8.29 us (3%)
    psum x4, waiting for transfers between devices, solve_block(): return lax.psum(partial_sum, 'prow')  131 us
    psum x1, waiting for transfers between devices, shards(): across = lax.psum(root_local, 'pcol')  35.1 us
    psum x1, waiting for transfers between devices, shards(): root_update = lax.psum(across, 'grid')  24.1 us
    ppermute x4, waiting for transfers between devices, from_partner(): lax.ppermute(shard, axis, [(i, i ^ 1 << bit) for i in range(lax.axis_size...  15.8 us
    dot_general x6, matrix products, shards(): jnp.dot(kept[source], factor_tile, preferred_element_type=jnp.float32)  14.9 us
    dot_general x4, matrix products, solve_block(): jnp.dot(residual.astype(jnp.bfloat16), inverse, preferred_element_type=jn...  9.38 us
    ppermute x4, starting transfers between devices, from_partner(): lax.ppermute(shard, axis, [(i, i ^ 1 << bit) for i in range(lax.axis_size...  8.05 us
  transfers between devices with their start and end apart: 10, of which 10 were waited for; matrix products, arithmetic and copies ran while one was open for 4% of the time, Pallas kernels for 0%

commit v1 on v0

--- a/solution.py
+++ b/solution.py
@@ -69,7 +69,7 @@
         root_local = root_local + jnp.dot(
             kept[source], factor_tile, preferred_element_type=jnp.float32
         )
-    across = lax.psum(root_local, "pcol")
+    across = jnp.sum(lax.all_gather(root_local, "pcol"), axis=0)
     root_update = lax.psum(across, "grid")
     root_solution = solve_block(root_rhs - root_update, root_inverse)
     return (jnp.stack(solved_all), root_solution)

time: 263 us -> 245 us (0.932)
  waiting for transfers between devices: 206 us -> 168 us
  blocking collectives: 0 us -> 19.8 us
    psum x1 -> x0, waiting for transfers between devices: 35.1 us -> none  [shards(): across = lax.psum(root_local, 'pcol')]
    all_gather x0 -> x1, blocking collectives: none -> 19.8 us  [shards(): across = jnp.sum(lax.all_gather(root_local, 'pcol'), axis=0)]
    psum x1, waiting for transfers between devices: 24.1 us -> 21 us  [shards(): root_update = lax.psum(across, 'grid')]
  transfers between devices with their start and end apart: 10 -> 9, of which waited for: 10 -> 9; matrix products, arithmetic and copies ran while one was open for 4% -> 5% of each run, Pallas kernels for 0% -> 0%
where the time goes in v1:
time: 245 us; the launch traced here: 244 us
  waiting for transfers between devices  168 us (69%)
  matrix products  29.4 us (12%)
  blocking collectives  19.8 us (8%)
  between operations  13.9 us (6%)
  starting transfers between devices  8.25 us (3%)
  other arithmetic  3.16 us (1%)
    psum x4, waiting for transfers between devices, solve_block(): return lax.psum(partial_sum, 'prow')  131 us
    psum x1, waiting for transfers between devices, shards(): root_update = lax.psum(across, 'grid')  21 us
    all_gather x1, blocking collectives, shards(): across = jnp.sum(lax.all_gather(root_local, 'pcol'), axis=0)  19.8 us
    ppermute x4, waiting for transfers between devices, from_partner(): lax.ppermute(shard, axis, [(i, i ^ 1 << bit) for i in range(lax.axis_size...  15.8 us
    dot_general x6, matrix products, shards(): jnp.dot(kept[source], factor_tile, preferred_element_type=jnp.float32)  14.9 us
    dot_general x4, matrix products, solve_block(): jnp.dot(residual.astype(jnp.bfloat16), inverse, preferred_element_type=jn...  9.39 us
    ppermute x4, starting transfers between devices, from_partner(): lax.ppermute(shard, axis, [(i, i ^ 1 << bit) for i in range(lax.axis_size...  8.05 us
    dot_general x6, matrix products, masked(): jnp.dot(row_select, mask.astype(jnp.float32))  5.13 us
  transfers between devices with their start and end apart: 9, of which 9 were waited for; matrix products, arithmetic and copies ran while one was open for 5% of the time, Pallas kernels for 0%

profile of v1, /device:TPU:0, one launch (start us, length us, event | category | flops | bytes accessed | tf_op | source)
XLA Modules:
  0.0 244.3 jit_solution(17635210643345866741)
XLA Ops:
  7.2 2.5 %fusion.22 = f32[64,768]{1,0:T(8,128)} fusion(bf16[3,768,768]{2,1,0:T(8,128)(2,1)} %param.10, f32[1,3,64,768]{3,2,1,0:T(8,128)} %param.8), kind=kOutput, calls=%fused_computation.28 | convolution fusion | flops 75497472 | bytes 1474560 | tf_op jit(solution)/shard_map/dot_general | solution.py:25
  11.1 34.6 %all-reduce.6.cloned.1.call-done = f32[64,768]{1,0:T(8,128)} async-done(((f32[64,768]{1,0:T(8,128)}), f32[64,768]{1,0:T(8,128)}) %all-reduce.6.cloned.1.call-update) | async-done | bytes 196624 | tf_op jit(solution)/shard_map/psum | solution.py:28
  45.7 2.1 fusion.11
  50.3 3.2 %collective-permute-done = f32[64,768]{1,0:T(8,128)S(1)} collective-permute-done((f32[64,768]{1,0:T(8,128)S(1)}, f32[64,768]{1,0:T(8,128)S(1)}, u32[]{:S(2)}, u32[]{:S(2)}) %collective-permute-start) | collective-permute-done | bytes 196640 | tf_op jit(solution)/shard_map/ppermute | solution.py:12
  53.6 2.5 %collective-permute-start.1 = (f32[64,768]{1,0:T(8,128)S(1)}, f32[64,768]{1,0:T(8,128)S(1)}, u32[]{:S(2)}, u32[]{:S(2)}) collective-permute-start(f32[64,768]{1,0:T(8,128)S(1)} %add.58), channel_id=1, source_target_pairs={{0,2},{1,3},{2,0},{3,1},{4,6},{5,7},{6,4},{7,5},{8,10},{9,11},{10,... | collective-permute-start | bytes 589832 | tf_op jit(solution)/shard_map/ppermute | solution.py:12
  56.0 1.7 fusion.37
  57.7 5.2 %collective-permute-done.1 = f32[64,768]{1,0:T(8,128)S(1)} collective-permute-done((f32[64,768]{1,0:T(8,128)S(1)}, f32[64,768]{1,0:T(8,128)S(1)}, u32[]{:S(2)}, u32[]{:S(2)}) %collective-permute-start.1) | collective-permute-done | bytes 196640 | tf_op jit(solution)/shard_map/ppermute | solution.py:12
  62.9 2.3 fusion.19
  66.3 32.6 %all-reduce.8.cloned.1.call-done = f32[64,768]{1,0:T(8,128)} async-done(((f32[64,768]{1,0:T(8,128)}), f32[64,768]{1,0:T(8,128)}) %all-reduce.8.cloned.1.call-update) | async-done | bytes 196624 | tf_op jit(solution)/shard_map/psum | solution.py:28
  98.8 2.8 %fusion.9 = f32[64,768]{1,0:T(8,128)} fusion(bf16[768,24]{1,0:T(8,128)(2,1)S(1)} %fusion.39, bf16[3,768,768]{2,1,0:T(8,128)(2,1)} %param.12, s32[768]{0:T(1024)S(1)} %copy-done.12, f32[64,768]{1,0:T(8,128)} %all-reduce.8.cloned.1.call-done), kind=kOutput, calls=%fused_computation.15 | convolution fusion | flops 104466432 | bytes 1612800 | tf_op jit(solution)/shard_map/dot_general | solution.py:58
  101.7 2.2 fusion.33
  106.4 3.2 %collective-permute-done.2 = f32[64,768]{1,0:T(8,128)S(1)} collective-permute-done((f32[64,768]{1,0:T(8,128)S(1)}, f32[64,768]{1,0:T(8,128)S(1)}, u32[]{:S(2)}, u32[]{:S(2)}) %collective-permute-start.2) | collective-permute-done | bytes 196640 | tf_op jit(solution)/shard_map/ppermute | solution.py:12
  110.6 2.5 %collective-permute-start.3 = (f32[64,768]{1,0:T(8,128)S(1)}, f32[64,768]{1,0:T(8,128)}, u32[]{:S(2)}, u32[]{:S(2)}) collective-permute-start(f32[64,768]{1,0:T(8,128)S(1)} %add.61), channel_id=1, source_target_pairs={{0,2},{1,3},{2,0},{3,1},{4,6},{5,7},{6,4},{7,5},{8,10},{9,11},{10,... | collective-permute-start | bytes 589832 | tf_op jit(solution)/shard_map/ppermute | solution.py:12
  113.0 2.8 %fusion.7 = f32[64,768]{1,0:T(8,128)} fusion(bf16[768,24]{1,0:T(8,128)(2,1)} %fusion.37, bf16[3,768,768]{2,1,0:T(8,128)(2,1)} %param.14, s32[768]{0:T(1024)} %add_select_fusion, f32[64,768]{1,0:T(8,128)S(1)} %copy-done.4), kind=kOutput, calls=%fused_computation.13 | convolution fusion | flops 104466432 | bytes 1773568 | tf_op jit(solution)/shard_map/dot_general | solution.py:69
  115.9 4.1 %collective-permute-done.3 = f32[64,768]{1,0:T(8,128)} collective-permute-done((f32[64,768]{1,0:T(8,128)S(1)}, f32[64,768]{1,0:T(8,128)}, u32[]{:S(2)}, u32[]{:S(2)}) %collective-permute-start.3) | collective-permute-done | bytes 196640 | tf_op jit(solution)/shard_map/ppermute | solution.py:12
  120.0 2.4 fusion.15
  122.5 2.0 fusion.34
  124.6 31.5 %all-reduce.10.cloned.1.call-done = f32[64,768]{1,0:T(8,128)} async-done(((f32[64,768]{1,0:T(8,128)}), f32[64,768]{1,0:T(8,128)}) %all-reduce.10.cloned.1.call-update) | async-done | bytes 196624 | tf_op jit(solution)/shard_map/psum | solution.py:28
  156.0 2.8 %fusion.35 = f32[64,768]{1,0:T(8,128)} fusion(f32[64,768]{1,0:T(8,128)S(1)} %fusion.34, bf16[768,24]{1,0:T(8,128)(2,1)S(1)} %copy-done.8, bf16[3,768,768]{2,1,0:T(8,128)(2,1)} %param.14, s32[768]{0:T(1024)S(1)} %copy-done.13, f32[64,768]{1,0:T(8,128)} %all-reduce.10.cloned.1.call-done), kind=kOutput, calls=%fused_computation.41 | convolution fusion | flops 104515584 | bytes 1809408 | tf_op jit(solution)/shard_map/dot_general | solution.py:69
  158.9 19.8 %all-gather = f32[256,768]{1,0:T(8,128)S(1)} all-gather(f32[64,768]{1,0:T(8,128)} %fusion.35), channel_id=2, replica_groups=mesh['grid'=2,'prow'=4,'pcol'=4] {'pcol'}, dimensions={0}, use_global_device_ids=true | all-gather | bytes 983040 | tf_op jit(solution)/shard_map/all_gather | solution.py:72
  179.5 21.0 %all-reduce.12.cloned.1.call-done = f32[64,768]{1,0:T(8,128)} async-done(((f32[64,768]{1,0:T(8,128)}), f32[64,768]{1,0:T(8,128)}) %all-reduce.12.cloned.1.call-update) | async-done | bytes 196624 | tf_op jit(solution)/shard_map/psum | solution.py:73
  200.4 2.2 fusion.62
  203.5 32.5 %all-reduce.14.cloned.1.call-done = f32[64,1536]{1,0:T(8,128)} async-done(((f32[64,1536]{1,0:T(8,128)}), f32[64,1536]{1,0:T(8,128)}) %all-reduce.14.cloned.1.call-update) | async-done | bytes 393232 | tf_op jit(solution)/shard_map/psum | solution.py:28
  236.0 1.8 copy.15
  (51 shorter events, 10.1 us)
Async XLA Ops:
  7.2 193.2 %copy-start = (bf16[768,1536]{1,0:T(8,128)(2,1)S(1)}, bf16[768,1536]{1,0:T(8,128)(2,1)}, u32[]{:S(2)}) copy-start(bf16[768,1536]{1,0:T(8,128)(2,1)} %param.11) | copy-start | bytes 7077892
  7.2 2.7 %copy-start.10 = (s32[3,6,24]{2,1,0:T(8,128)S(1)}, s32[3,6,24]{2,1,0:T(8,128)}, u32[]{:S(2)}) copy-start(s32[3,6,24]{2,1,0:T(8,128)} %param.13) | copy-start | bytes 5188
  7.2 38.5 %all-reduce.6.cloned.1.call-start = ((), (), s32[]{:S(2)}) async-start(), calls=%async_computation | async-start | bytes 393216 | tf_op jit(solution)/shard_map/psum | solution.py:28
  9.8 89.0 %all-reduce.8.cloned.1.call-start = ((), (), s32[]{:S(2)}) async-start(), calls=%async_computation.1 | async-start | bytes 393216 | tf_op jit(solution)/shard_map/psum | solution.py:28
  11.1 51.9 %copy-start.1 = (f32[1,3,64,768]{3,2,1,0:T(8,128)S(1)}, f32[1,3,64,768]{3,2,1,0:T(8,128)}, u32[]{:S(2)}) copy-start(f32[1,3,64,768]{3,2,1,0:T(8,128)} %param.8) | copy-start | bytes 1769476
  47.8 5.7 %collective-permute-start = (f32[64,768]{1,0:T(8,128)S(1)}, f32[64,768]{1,0:T(8,128)S(1)}, u32[]{:S(2)}, u32[]{:S(2)}) collective-permute-start(f32[64,768]{1,0:T(8,128)S(1)} %fusion.11), channel_id=1, source_target_pairs={{0,1},{1,0},{2,3},{3,2},{4,5},{5,4},{6,7},{7,6},{8,9},{9,8},{10,11... | collective-permute-start | bytes 589832 | tf_op jit(solution)/shard_map/ppermute | solution.py:12
  53.6 11.7 %copy-start.11 = (s32[3,6,24]{2,1,0:T(8,128)S(1)}, s32[3,6,24]{2,1,0:T(8,128)}, u32[]{:S(2)}) copy-start(s32[3,6,24]{2,1,0:T(8,128)} %param.15) | copy-start | bytes 5188
  53.6 9.4 %collective-permute-start.1 = (f32[64,768]{1,0:T(8,128)S(1)}, f32[64,768]{1,0:T(8,128)S(1)}, u32[]{:S(2)}, u32[]{:S(2)}) collective-permute-start(f32[64,768]{1,0:T(8,128)S(1)} %add.58), channel_id=1, source_target_pairs={{0,2},{1,3},{2,0},{3,1},{4,6},{5,7},{6,4},{7,5},{8,10},{9,11},{10,... | collective-permute-start | bytes 589832 | tf_op jit(solution)/shard_map/ppermute | solution.py:12
  57.7 41.1 %copy-start.12 = (s32[768]{0:T(1024)S(1)}, s32[768]{0:T(1024)}, u32[]{:S(2)}) copy-start(s32[768]{0:T(1024)} %add_select_fusion) | copy-start | bytes 9220
  65.2 36.4 %copy-start.3 = (f32[64,768]{1,0:T(8,128)S(1)}, f32[64,768]{1,0:T(8,128)}, u32[]{:S(2)}) copy-start(f32[64,768]{1,0:T(8,128)} %all-reduce.6.cloned.1.call-done) | copy-start | bytes 589828
  65.2 90.8 %all-reduce.10.cloned.1.call-start = ((), (), s32[]{:S(2)}) async-start(), calls=%async_computation.2 | async-start | bytes 393216 | tf_op jit(solution)/shard_map/psum | solution.py:28
  101.7 11.4 %copy-start.4 = (f32[64,768]{1,0:T(8,128)S(1)}, f32[64,768]{1,0:T(8,128)}, u32[]{:S(2)}) copy-start(f32[64,768]{1,0:T(8,128)} %all-reduce.8.cloned.1.call-done) | copy-start | bytes 589828
  103.9 2.5 %copy-start.9 = (f32[64,768]{1,0:T(8,128)}, f32[64,768]{1,0:T(8,128)S(1)}, u32[]{:S(2)}) copy-start(f32[64,768]{1,0:T(8,128)S(1)} %fusion.33) | copy-start | bytes 589828
  103.9 5.7 %collective-permute-start.2 = (f32[64,768]{1,0:T(8,128)S(1)}, f32[64,768]{1,0:T(8,128)S(1)}, u32[]{:S(2)}, u32[]{:S(2)}) collective-permute-start(f32[64,768]{1,0:T(8,128)S(1)} %fusion.33), channel_id=1, source_target_pairs={{0,1},{1,0},{2,3},{3,2},{4,5},{5,4},{6,7},{7,6},{8,9},{9,8},{10,11... | collective-permute-start | bytes 589832 | tf_op jit(solution)/shard_map/ppermute | solution.py:12
  110.6 9.5 %collective-permute-start.3 = (f32[64,768]{1,0:T(8,128)S(1)}, f32[64,768]{1,0:T(8,128)}, u32[]{:S(2)}, u32[]{:S(2)}) collective-permute-start(f32[64,768]{1,0:T(8,128)S(1)} %add.61), channel_id=1, source_target_pairs={{0,2},{1,3},{2,0},{3,1},{4,6},{5,7},{6,4},{7,5},{8,10},{9,11},{10,... | collective-permute-start | bytes 589832 | tf_op jit(solution)/shard_map/ppermute | solution.py:12
  115.9 6.6 %copy-start.7 = (bf16[768,24]{1,0:T(8,128)(2,1)S(1)}, bf16[768,24]{1,0:T(8,128)(2,1)}, u32[]{:S(2)}) copy-start(bf16[768,24]{1,0:T(8,128)(2,1)} %fusion.38) | copy-start | bytes 110596
  115.9 6.6 %copy-start.13 = (s32[768]{0:T(1024)S(1)}, s32[768]{0:T(1024)}, u32[]{:S(2)}) copy-start(s32[768]{0:T(1024)} %add_select_fusion) | copy-start | bytes 9220
  122.4 33.6 %copy-start.8 = (bf16[768,24]{1,0:T(8,128)(2,1)S(1)}, bf16[768,24]{1,0:T(8,128)(2,1)}, u32[]{:S(2)}) copy-start(bf16[768,24]{1,0:T(8,128)(2,1)} %fusion.36) | copy-start | bytes 110596
  122.4 78.0 %all-reduce.12.cloned.1.call-start = ((), (), s32[]{:S(2)}) async-start(), calls=%async_computation.3 | async-start | bytes 393216 | tf_op jit(solution)/shard_map/psum | solution.py:73
  158.9 41.5 %copy-start.2 = (f32[64,768]{1,0:T(8,128)S(1)}, f32[64,768]{1,0:T(8,128)}, u32[]{:S(2)}) copy-start(f32[64,768]{1,0:T(8,128)} %param.9) | copy-start | bytes 589828
  179.4 23.3 %copy-start.5 = (f32[64,768]{1,0:T(8,128)S(1)}, f32[64,768]{1,0:T(8,128)}, u32[]{:S(2)}) copy-start(f32[64,768]{1,0:T(8,128)} %all-reduce.8.cloned.1.call-done) | copy-start | bytes 589828
  179.4 23.3 %copy-start.6 = (f32[64,768]{1,0:T(8,128)S(1)}, f32[64,768]{1,0:T(8,128)}, u32[]{:S(2)}) copy-start(f32[64,768]{1,0:T(8,128)} %all-reduce.10.cloned.1.call-done) | copy-start | bytes 589828
  179.4 56.6 %all-reduce.14.cloned.1.call-start = ((), (), s32[]{:S(2)}) async-start(), calls=%async_computation.4 | async-start | bytes 786432 | tf_op jit(solution)/shard_map/psum | solution.py:28
Sparse Core Ops, SparseCore 0:
  10.9 34.7 all-reduce.5
  65.3 33.4 all-reduce.7
  122.6 33.4 all-reduce.9
  179.5 20.8 all-reduce.11
  203.2 32.7 all-reduce.13
